TPU v7x, 32 devices: a whole 2x2x4 slice. The times are simulated.
32 devices in a mesh: energy: 4 (over z), orb: 4 (over y, x), kpt: 2 (over core).
Axes of the slice: x: 2, y: 2, z: 4, core: 2. Of those that a mesh axis runs over, the one named last changes fastest.
Arguments:
- lesser: bfloat16 [2, 4, 16, 1, 512, 512], P(None, 'energy', 'kpt', None, None, 'orb'), may hold values from -6 to 6
- coupling: bfloat16 [2, 16, 512, 512], P(None, None, None, 'orb'), may hold values from -0.046875 to 0.046875
- transfer_map: int32 [16, 16], replicated, may hold values from 0 to 15, as said below
Outputs:
- sigma: bfloat16 [2, 4, 16, 1, 512, 512], P(None, None, 'kpt', None, 'energy', 'orb')
Inputs may be any that keep to these rules, and one draw needn't show every extreme that they name: transfer_map[k, p] is the index of the momentum transfer k - p: each row and each column holds every number of 0 to 15 once.
All inputs are finite; a program needn't handle non-finite values.
Results may differ from a plain program's by a relative error of at most 0.001.
Values may be sent and summed in bfloat16 or wider, within the bound.
A program may use at most 128 MiB of HBM per device.

v0:
```python
import functools

import jax
import jax.numpy as jnp
from jax import lax
from jax.experimental import pallas as pl
from jax.experimental.pallas import tpu as pltpu
from jax.sharding import PartitionSpec as P

MESH = pl.DeviceIdType.MESH
DA, DB, P0, PX, PY, PD = range(6)
AHEAD = 1


def complex_terms(green, selected):
    real_out = jnp.einsum(
        "prm,tpmj->trj", green[0], selected[0], preferred_element_type=jnp.float32
    ) - jnp.einsum("prm,tpmj->trj", green[1], selected[1], preferred_element_type=jnp.float32)
    imag_out = jnp.einsum(
        "prm,tpmj->trj", green[0], selected[1], preferred_element_type=jnp.float32
    ) + jnp.einsum("prm,tpmj->trj", green[1], selected[0], preferred_element_type=jnp.float32)
    return (real_out, imag_out)


def per_device_general(lesser, coupling, transfer_map):
    regrouped = lax.all_to_all(lesser, "energy", split_axis=4, concat_axis=1, tiled=True)
    gathered = lax.all_gather(regrouped, "orb", axis=5, tiled=True)
    energies = gathered.shape[1]
    local_points = gathered.shape[2]
    layers = gathered.shape[3]
    tile = gathered.shape[4]
    width = gathered.shape[5]
    out_cols = coupling.shape[3]
    row_count = energies * layers * tile
    first_point = lax.axis_index("kpt") * local_points
    reordered = jnp.moveaxis(gathered, 2, 1).reshape(2, local_points, row_count, width)
    my_columns = lax.dynamic_slice_in_dim(transfer_map, first_point, local_points, 1)
    selected = jnp.take(coupling, my_columns, axis=1)
    real_out, imag_out = complex_terms(reordered, selected)
    mine = lax.psum_scatter(
        jnp.stack([real_out, imag_out], axis=1), "kpt", scatter_dimension=0, tiled=True
    )
    summed = jnp.moveaxis(mine, 1, 0)
    result = summed.astype(jnp.bfloat16).reshape(2, local_points, energies, layers, tile, out_cols)
    return jnp.moveaxis(result, 1, 2)


def kernel(nz, map_ref, lesser, coupling, out, g, u, acc, zsend, zrecv, osend, orecv, send, recv, local_sem, u_sem):
    points = lesser.shape[2]
    width = lesser.shape[5]
    tile = g.shape[5]
    rows = nz * tile
    e = lax.axis_index("energy")
    o = lax.axis_index("orb")
    c = lax.axis_index("kpt")
    ox = o + 1 - 2 * lax.rem(o, 2)
    oy = lax.rem(o + 2, 4)
    od = 3 - o
    cp = 1 - c

    def to_energy(d):
        return lax.rem(e + d, nz)

    def from_energy(d):
        return lax.rem(e + nz - d, nz)

    def own_rows(s, z):
        return lesser.at[:, 0, s, 0, pl.ds(pl.multiple_of(z * tile, tile), tile), :]

    def z_copy(d, s, owner, target):
        return pltpu.make_async_remote_copy(
            src_ref=own_rows(s, target),
            dst_ref=g.at[c, o, :, s, owner],
            send_sem=zsend.at[d - 1, s],
            recv_sem=zrecv.at[d - 1, s],
            device_id={"energy": target},
            device_id_type=MESH,
        )

    def local_copy(s):
        return pltpu.make_async_copy(own_rows(s, e), g.at[c, o, :, s, e], local_sem.at[s])

    def move(kind, s, ref, target):
        return pltpu.make_async_remote_copy(
            src_ref=ref,
            dst_ref=ref,
            send_sem=send.at[kind, s],
            recv_sem=recv.at[kind, s],
            device_id=target,
            device_id_type=MESH,
        )

    def own_copy(way, d, s):
        owner = from_energy(d)
        tile_ref = g.at[c, o, :, s, owner]
        return pltpu.make_async_remote_copy(
            src_ref=own_rows(s, e) if d == 0 else tile_ref,
            dst_ref=tile_ref,
            send_sem=osend.at[way, d, s],
            recv_sem=orecv.at[way, d, s],
            device_id=(to_x, to_y)[way],
            device_id_type=MESH,
        )

    def wait_own(way, s):
        for d in range(nz):
            tile_ref = g.at[c, (ox, oy)[way], :, s, from_energy(d)]
            pltpu.make_async_remote_copy(
                src_ref=tile_ref,
                dst_ref=tile_ref,
                send_sem=osend.at[way, d, s],
                recv_sem=orecv.at[way, d, s],
                device_id=(to_x, to_y)[way],
                device_id_type=MESH,
            ).wait_recv()

    def block(k, q, s):
        return g.at[k, q, :, s]

    def half(q, part, s):
        return g.at[c, q, part, s]

    to_x, to_y, to_peer = {"orb": ox}, {"orb": oy}, {"kpt": cp}

    def outgoing(kind, s):
        refs = {
            P0: lambda: block(c, o, s),
            DA: lambda: half(ox, 0, s),
            PX: lambda: block(c, ox, s),
            DB: lambda: half(oy, 1, s),
            PY: lambda: block(c, oy, s),
            PD: lambda: block(c, od, s),
        }
        return move(kind, s, refs[kind](), {DA: to_y, DB: to_x}.get(kind, to_peer))

    def incoming(kind, s):
        refs = {
            DA: lambda: half(od, 0, s),
            DB: lambda: half(od, 1, s),
            P0: lambda: block(cp, o, s),
            PX: lambda: block(cp, ox, s),
            PY: lambda: block(cp, oy, s),
            PD: lambda: block(cp, od, s),
        }
        return move(kind, s, refs[kind](), {DA: to_y, DB: to_x}.get(kind, to_peer))

    def locals_start(s, _):
        local_copy(s).start()
        return 0

    lax.fori_loop(0, points, locals_start, 0)
    u_copy = pltpu.make_async_copy(coupling, u, u_sem)
    u_copy.start()

    barrier = pltpu.get_barrier_semaphore()
    for d in range(1, nz):
        pl.semaphore_signal(barrier, inc=1, device_id={"energy": to_energy(d)}, device_id_type=MESH)
    for target in (to_x, to_y, to_peer):
        pl.semaphore_signal(barrier, inc=1, device_id=target, device_id_type=MESH)
    pl.semaphore_wait(barrier, nz - 1 + 3)

    def z_start(s, _):
        for d in range(1, nz):
            z_copy(d, s, e, to_energy(d)).start()
        own_copy(0, 0, s).start()
        own_copy(1, 0, s).start()
        return 0

    lax.fori_loop(0, points, z_start, 0)

    def clear(t, _):
        acc[t] = jnp.zeros(acc.shape[1:], acc.dtype)
        return 0

    lax.fori_loop(0, points, clear, 0)
    u_copy.wait()

    def multiply(chunks, s):
        def one(t, _):
            lhs, rhs = [], []
            for k, q in chunks:
                lhs.append(g[k, q, 0, s].reshape(rows, width))
                lhs.append(g[k, q, 1, s].reshape(rows, width))
                index = map_ref[c * points + t, k * points + s]
                at = pl.ds(pl.multiple_of(q * width, width), width)
                ur = u[0, index, at, :]
                ui = u[1, index, at, :]
                rhs.append(jnp.concatenate([ur, ui], axis=1))
                rhs.append(jnp.concatenate([-ui, ur], axis=1))
            acc[t] += jnp.dot(
                jnp.concatenate(lhs, axis=1),
                jnp.concatenate(rhs, axis=0),
                preferred_element_type=jnp.float32,
            )
            return 0

        lax.fori_loop(0, points, one, 0, unroll=True)

    def drain(s):
        for d in range(1, nz):
            z_copy(d, s, e, to_energy(d)).wait_send()
        for d in range(nz):
            own_copy(0, d, s).wait_send()
            own_copy(1, d, s).wait_send()
        for kind in range(6):
            outgoing(kind, s).wait_send()

    def lagged(s, lag):
        return pl.when((s >= lag) & (s < points + lag))

    def tick(s, _):
        @lagged(s, 0)
        def _():
            for d in range(1, nz):
                z_copy(d, s, from_energy(d), e).wait_recv()
                own_copy(0, d, s).start()
                own_copy(1, d, s).start()
            local_copy(s).wait()
            outgoing(P0, s).start()

        @lagged(s, AHEAD)
        def _():
            r = s - AHEAD
            wait_own(0, r)
            outgoing(DA, r).start()
            outgoing(PX, r).start()
            wait_own(1, r)
            outgoing(DB, r).start()
            outgoing(PY, r).start()

        @lagged(s, AHEAD)
        def _():
            r = s - AHEAD
            incoming(P0, r).wait_recv()
            multiply(((c, o), (cp, o)), r)
            multiply(((c, ox), (c, oy)), r)

        @lagged(s, AHEAD + 1)
        def _():
            r = s - AHEAD - 1
            incoming(DA, r).wait_recv()
            incoming(DB, r).wait_recv()
            outgoing(PD, r).start()

        @lagged(s, AHEAD + 1)
        def _():
            r = s - AHEAD - 1
            incoming(PX, r).wait_recv()
            incoming(PY, r).wait_recv()
            multiply(((cp, ox), (cp, oy)), r)

        @lagged(s, AHEAD + 2)
        def _():
            r = s - AHEAD - 2
            incoming(PD, r).wait_recv()
            multiply(((c, od), (cp, od)), r)
            drain(r)

        return 0

    lax.fori_loop(0, points + AHEAD + 2, tick, 0)

    def finish(t, _):
        for k in range(nz):
            for part in range(2):
                values = acc[t, k * tile : (k + 1) * tile, part * width : (part + 1) * width]
                out[part, k, t, 0] = values.astype(out.dtype)
        return 0

    lax.fori_loop(0, points, finish, 0, unroll=True)


def per_device_fused(nz, lesser, coupling, transfer_map):
    points = lesser.shape[2]
    tile = lesser.shape[4] // nz
    width = lesser.shape[5]
    out_cols = coupling.shape[3]
    dma = pltpu.SemaphoreType.DMA
    return pl.pallas_call(
        functools.partial(kernel, nz),
        out_shape=jax.ShapeDtypeStruct((2, nz, points, 1, tile, out_cols), jnp.bfloat16),
        in_specs=[
            pl.BlockSpec(memory_space=pltpu.SMEM),
            pl.BlockSpec(memory_space=pl.ANY),
            pl.BlockSpec(memory_space=pl.ANY),
        ],
        out_specs=pl.BlockSpec(memory_space=pltpu.VMEM),
        scratch_shapes=[
            pltpu.VMEM((2, 4, 2, points, nz, tile, width), lesser.dtype),
            pltpu.VMEM(coupling.shape, coupling.dtype),
            pltpu.VMEM((points, nz * tile, 2 * out_cols), jnp.float32),
            dma((nz - 1, points)),
            dma((nz - 1, points)),
            dma((2, nz, points)),
            dma((2, nz, points)),
            dma((6, points)),
            dma((6, points)),
            dma((points,)),
            dma(()),
        ],
        compiler_params=pltpu.CompilerParams(
            collective_id=0, has_side_effects=True, vmem_limit_bytes=56 * 1024 * 1024
        ),
    )(transfer_map, lesser, coupling)


def solution(mesh):
    in_specs = (P(None, "energy", "kpt", None, None, "orb"), P(None, None, None, "orb"), P())
    out_specs = P(None, None, "kpt", None, "energy", "orb")
    nz = mesh.shape["energy"]

    def per_device(lesser, coupling, transfer_map):
        shape = lesser.shape
        fused = (
            mesh.shape["orb"] == 4
            and mesh.shape["kpt"] == 2
            and nz > 1
            and shape[1] == 1
            and shape[3] == 1
            and shape[5] == coupling.shape[3] == 128
            and shape[4] == nz * 128
        )
        if fused:
            return per_device_fused(nz, lesser, coupling, transfer_map)
        return per_device_general(lesser, coupling, transfer_map)

    return jax.shard_map(
        per_device, mesh=mesh, in_specs=in_specs, out_specs=out_specs, check_vma=False
    )
```

profile of v0, /device:TPU:0, one launch (start us, length us, event | category | flops | bytes accessed | tf_op | source)
XLA Modules:
  0.0 88.3 jit_solution(1745374349960501768)
XLA Ops:
  0.0 85.1 %shard_map.37 = bf16[2,4,8,1,128,128]{5,4,3,2,1,0:T(8,128)(2,1)} custom-call(s32[16,16]{1,0:T(8,128)} %map_ref.1, bf16[2,1,8,1,512,128]{5,4,3,2,1,0:T(8,128)(2,1)} %lesser.1, bf16[2,16,512,128]{3,2,1,0:T(8,128)(2,1)} %coupling.1), custom_call_target="tpu_custom_call" | custom-call | tf_op jit(solution)/shard_map/pallas_call | solution.py:279
  85.1 3.2 %copy.5 = bf16[2,4,8,1,128,128]{5,4,3,2,1,0:T(8,128)(2,1)} copy(bf16[2,4,8,1,128,128]{5,4,3,2,1,0:T(8,128)(2,1)} %shard_map.37) | data formatting | bytes 4194304
where the time goes:
time: 88.6 us; the launch traced here: 88.3 us
  Pallas kernels  85.1 us (96%)
  local copies, waits for them, and re-layouts  3.16 us (4%)
    pallas_call x1, Pallas kernels, per_device_fused(): pl.pallas_call(functools.partial(kernel, nz), out_shape=jax.ShapeDtypeStr...  85.1 us
    unnamed x1, local copies, waits for them, and re-layouts  3.16 us

commit v1 on v0

v1 whole, which is shorter than its diff:
```python
import functools

import jax
import jax.numpy as jnp
from jax import lax
from jax.experimental import pallas as pl
from jax.experimental.pallas import tpu as pltpu
from jax.sharding import PartitionSpec as P

MESH = pl.DeviceIdType.MESH
DA, DB, P0, PX, PY, PD = range(6)
RELAY, DIAG, MULTIPLY = 2, 4, 5


def complex_terms(green, selected):
    real_out = jnp.einsum(
        "prm,tpmj->trj", green[0], selected[0], preferred_element_type=jnp.float32
    ) - jnp.einsum("prm,tpmj->trj", green[1], selected[1], preferred_element_type=jnp.float32)
    imag_out = jnp.einsum(
        "prm,tpmj->trj", green[0], selected[1], preferred_element_type=jnp.float32
    ) + jnp.einsum("prm,tpmj->trj", green[1], selected[0], preferred_element_type=jnp.float32)
    return (real_out, imag_out)


def per_device_general(lesser, coupling, transfer_map):
    regrouped = lax.all_to_all(lesser, "energy", split_axis=4, concat_axis=1, tiled=True)
    gathered = lax.all_gather(regrouped, "orb", axis=5, tiled=True)
    energies = gathered.shape[1]
    local_points = gathered.shape[2]
    layers = gathered.shape[3]
    tile = gathered.shape[4]
    width = gathered.shape[5]
    out_cols = coupling.shape[3]
    row_count = energies * layers * tile
    first_point = lax.axis_index("kpt") * local_points
    reordered = jnp.moveaxis(gathered, 2, 1).reshape(2, local_points, row_count, width)
    my_columns = lax.dynamic_slice_in_dim(transfer_map, first_point, local_points, 1)
    selected = jnp.take(coupling, my_columns, axis=1)
    real_out, imag_out = complex_terms(reordered, selected)
    mine = lax.psum_scatter(
        jnp.stack([real_out, imag_out], axis=1), "kpt", scatter_dimension=0, tiled=True
    )
    summed = jnp.moveaxis(mine, 1, 0)
    result = summed.astype(jnp.bfloat16).reshape(2, local_points, energies, layers, tile, out_cols)
    return jnp.moveaxis(result, 1, 2)


def kernel(nz, map_hbm, lesser, coupling, out, g, u, acc, map_ref, zsend, zrecv, osend, orecv, send, recv, local_sem, u_sem, map_sem):
    points = lesser.shape[2]
    width = lesser.shape[5]
    tile = g.shape[5]
    ticks = nz * points
    e = lax.axis_index("energy")
    o = lax.axis_index("orb")
    c = lax.axis_index("kpt")
    ox = o + 1 - 2 * lax.rem(o, 2)
    oy = lax.rem(o + 2, 4)
    od = 3 - o
    cp = 1 - c
    to_x, to_y, to_peer = {"orb": ox}, {"orb": oy}, {"kpt": cp}

    def offset(i):
        phase = lax.div(i, points)
        near = lax.div(phase + 1, 2)
        return lax.select(lax.rem(phase, 2) == 1, near, lax.rem(nz - lax.div(phase, 2), nz))

    def point(i):
        return lax.rem(i, points)

    def to_energy(d):
        return lax.rem(e + d, nz)

    def owner(i):
        return lax.rem(e + nz - offset(i), nz)

    def own_rows(s, z):
        return lesser.at[:, 0, s, 0, pl.ds(pl.multiple_of(z * tile, tile), tile), :]

    def block(k, q, i):
        return g.at[k, q, :, point(i), owner(i)]

    def half(q, part, i):
        return g.at[c, q, part, point(i), owner(i)]

    def z_copy(i):
        target = to_energy(offset(i))
        return pltpu.make_async_remote_copy(
            src_ref=own_rows(point(i), target),
            dst_ref=g.at[c, o, :, point(i), e],
            send_sem=zsend.at[i - points],
            recv_sem=zrecv.at[i - points],
            device_id={"energy": target},
            device_id_type=MESH,
        )

    def z_arrival(i):
        tile_ref = block(c, o, i)
        return pltpu.make_async_remote_copy(
            src_ref=tile_ref,
            dst_ref=tile_ref,
            send_sem=zsend.at[i - points],
            recv_sem=zrecv.at[i - points],
            device_id={"energy": owner(i)},
            device_id_type=MESH,
        )

    def local_copy(s):
        return pltpu.make_async_copy(own_rows(s, e), g.at[c, o, :, s, e], local_sem.at[s])

    def own_copy(way, i, src, dst):
        return pltpu.make_async_remote_copy(
            src_ref=src,
            dst_ref=dst,
            send_sem=osend.at[way, i],
            recv_sem=orecv.at[way, i],
            device_id=(to_x, to_y)[way],
            device_id_type=MESH,
        )

    def own_arrival(way, i):
        tile_ref = block(c, (ox, oy)[way], i)
        return own_copy(way, i, tile_ref, tile_ref)

    def move(kind, i, ref):
        return pltpu.make_async_remote_copy(
            src_ref=ref,
            dst_ref=ref,
            send_sem=send.at[kind, i],
            recv_sem=recv.at[kind, i],
            device_id={DA: to_y, DB: to_x}.get(kind, to_peer),
            device_id_type=MESH,
        )

    def outgoing(kind, i):
        refs = {
            P0: lambda: block(c, o, i),
            DA: lambda: half(ox, 0, i),
            PX: lambda: block(c, ox, i),
            DB: lambda: half(oy, 1, i),
            PY: lambda: block(c, oy, i),
            PD: lambda: block(c, od, i),
        }
        return move(kind, i, refs[kind]())

    def incoming(kind, i):
        refs = {
            DA: lambda: half(od, 0, i),
            DB: lambda: half(od, 1, i),
            P0: lambda: block(cp, o, i),
            PX: lambda: block(cp, ox, i),
            PY: lambda: block(cp, oy, i),
            PD: lambda: block(cp, od, i),
        }
        return move(kind, i, refs[kind]())

    def locals_start(s, _):
        local_copy(s).start()
        return 0

    barrier = pltpu.get_barrier_semaphore()
    for d in range(1, nz):
        pl.semaphore_signal(barrier, inc=1, device_id={"energy": to_energy(d)}, device_id_type=MESH)
    for target in (to_x, to_y, to_peer):
        pl.semaphore_signal(barrier, inc=1, device_id=target, device_id_type=MESH)
    lax.fori_loop(0, points, locals_start, 0)
    map_copy = pltpu.make_async_copy(map_hbm, map_ref, map_sem)
    map_copy.start()
    u_copy = pltpu.make_async_copy(coupling, u, u_sem)
    u_copy.start()
    pl.semaphore_wait(barrier, nz - 1 + 3)

    def first_start(s, _):
        dst = g.at[c, o, :, s, e]
        own_copy(0, s, own_rows(s, e), dst).start()
        own_copy(1, s, own_rows(s, e), dst).start()
        z_copy(points + s).start()
        return 0

    def z_start(i, _):
        z_copy(i).start()
        return 0

    lax.fori_loop(0, points, first_start, 0)
    lax.fori_loop(2 * points, ticks, z_start, 0)

    acc[...] = jnp.zeros(acc.shape, acc.dtype)
    map_copy.wait()
    u_copy.wait()

    def multiply(chunks, i, store):
        s = point(i)
        z = owner(i)

        def one(t, _):
            lhs, rhs = [], []
            for k, q in chunks:
                lhs.append(g[k, q, 0, s, z])
                lhs.append(g[k, q, 1, s, z])
                index = map_ref[c * points + t, k * points + s]
                at = pl.ds(pl.multiple_of(q * width, width), width)
                ur = u[0, index, at, :]
                ui = u[1, index, at, :]
                rhs.append(jnp.concatenate([ur, ui], axis=1))
                rhs.append(jnp.concatenate([-ui, ur], axis=1))
            store(
                t,
                acc[t]
                + jnp.dot(
                    jnp.concatenate(lhs, axis=1),
                    jnp.concatenate(rhs, axis=0),
                    preferred_element_type=jnp.float32,
                ),
            )
            return 0

        lax.fori_loop(0, points, one, 0, unroll=True)

    def add(t, values):
        acc[t] = values

    def write(z):
        def store(t, values):
            for part in range(2):
                out[part, z, t, 0] = values[:, part * width : (part + 1) * width].astype(out.dtype)

        return store

    def drain(i):
        @pl.when(i >= points)
        def _():
            z_copy(i).wait_send()

        own_arrival(0, i).wait_send()
        own_arrival(1, i).wait_send()
        for kind in range(6):
            outgoing(kind, i).wait_send()

    def lagged(i, lag):
        return pl.when((i >= lag) & (i < ticks + lag))

    early = ((c, o), (cp, o), (c, ox), (cp, ox), (c, oy), (cp, oy))
    late = ((c, od), (cp, od))

    def arrive(i, kinds):
        for kind in kinds:
            incoming(kind, i).wait_recv()

    def relay(r):
        own_arrival(0, r).wait_recv()
        outgoing(DA, r).start()
        outgoing(PX, r).start()
        own_arrival(1, r).wait_recv()
        outgoing(DB, r).start()
        outgoing(PY, r).start()

    def diagonal(r):
        arrive(r, (DA, DB))
        outgoing(PD, r).start()

    def tick(i, _):
        @pl.when(i < points)
        def _():
            local_copy(point(i)).wait()
            outgoing(P0, i).start()

        @pl.when((i >= points) & (i < ticks))
        def _():
            z_arrival(i).wait_recv()
            for way in range(2):
                own_copy(way, i, block(c, o, i), block(c, o, i)).start()
            outgoing(P0, i).start()

        @lagged(i, RELAY)
        def _():
            relay(i - RELAY)

        @lagged(i, DIAG)
        def _():
            diagonal(i - DIAG)

        @pl.when(i >= MULTIPLY)
        def _():
            r = i - MULTIPLY
            arrive(r, (P0, PX, PY, PD))
            multiply(early + late, r, add)
            drain(r)

            @pl.when(point(r) == points - 1)
            def _():
                z = owner(r)

                def flush(t, _):
                    write(z)(t, acc[t])
                    acc[t] = jnp.zeros(acc.shape[1:], acc.dtype)
                    return 0

                lax.fori_loop(0, points, flush, 0, unroll=True)

        return 0

    lax.fori_loop(0, ticks + MULTIPLY - 1, tick, 0)
    last = ticks - 1
    arrive(last, (P0, PX, PY))
    multiply(early, last, add)
    arrive(last, (PD,))
    multiply(late, last, write(owner(last)))
    drain(last)


def per_device_fused(nz, lesser, coupling, transfer_map):
    points = lesser.shape[2]
    tile = lesser.shape[4] // nz
    width = lesser.shape[5]
    out_cols = coupling.shape[3]
    dma = pltpu.SemaphoreType.DMA
    lesser, coupling, transfer_map = (
        pltpu.with_memory_space_constraint(x, pltpu.HBM) for x in (lesser, coupling, transfer_map)
    )
    return pl.pallas_call(
        functools.partial(kernel, nz),
        out_shape=jax.ShapeDtypeStruct((2, nz, points, 1, tile, out_cols), jnp.bfloat16),
        in_specs=[pl.BlockSpec(memory_space=pltpu.HBM)] * 3,
        out_specs=pl.BlockSpec(memory_space=pltpu.VMEM),
        scratch_shapes=[
            pltpu.VMEM((2, 4, 2, points, nz, tile, width), lesser.dtype),
            pltpu.VMEM(coupling.shape, coupling.dtype),
            pltpu.VMEM((points, tile, 2 * out_cols), jnp.float32),
            pltpu.SMEM(transfer_map.shape, transfer_map.dtype),
            dma(((nz - 1) * points,)),
            dma(((nz - 1) * points,)),
            dma((2, nz * points)),
            dma((2, nz * points)),
            dma((6, nz * points)),
            dma((6, nz * points)),
            dma((points,)),
            dma(()),
            dma(()),
        ],
        compiler_params=pltpu.CompilerParams(
            collective_id=0, has_side_effects=True, vmem_limit_bytes=40 * 1024 * 1024
        ),
    )(transfer_map, lesser, coupling)


def solution(mesh):
    in_specs = (P(None, "energy", "kpt", None, None, "orb"), P(None, None, None, "orb"), P())
    out_specs = P(None, None, "kpt", None, "energy", "orb")
    nz = mesh.shape["energy"]

    def per_device(lesser, coupling, transfer_map):
        shape = lesser.shape
        fused = (
            mesh.shape["orb"] == 4
            and mesh.shape["kpt"] == 2
            and nz > 1
            and shape[1] == 1
            and shape[3] == 1
            and shape[5] == coupling.shape[3] == 128
            and shape[4] == nz * 128
        )
        if fused:
            return per_device_fused(nz, lesser, coupling, transfer_map)
        return per_device_general(lesser, coupling, transfer_map)

    return jax.shard_map(
        per_device, mesh=mesh, in_specs=in_specs, out_specs=out_specs, check_vma=False
    )
```

time: 88.6 us -> 90.9 us (1.026)
  Pallas kernels: 85.1 us -> 89.4 us
  local copies, waits for them, and re-layouts: 3.16 us -> 1.32 us
    pallas_call x1, Pallas kernels: 85.1 us -> 89.4 us  [per_device_fused(): pl.pallas_call(functools.partial(kernel, nz), out_shape=jax.ShapeDtypeStr...]
    unnamed x1, local copies, waits for them, and re-layouts: 3.16 us -> 1.32 us
where the time goes in v1:
time: 90.9 us; the launch traced here: 90.7 us
  Pallas kernels  89.4 us (98%)
  local copies, waits for them, and re-layouts  1.32 us (1%)
    pallas_call x1, Pallas kernels, per_device_fused(): pl.pallas_call(functools.partial(kernel, nz), out_shape=jax.ShapeDtypeStr...  89.4 us

profile of v1, /device:TPU:0, one launch (start us, length us, event | category | flops | bytes accessed | tf_op | source)
XLA Modules:
  0.0 90.7 jit_solution(8913934297742805258)
XLA Ops:
  0.0 89.4 %shard_map.37 = bf16[2,4,8,1,128,128]{5,4,3,2,1,0:T(8,128)(2,1)S(1)} custom-call(s32[16,16]{1,0:T(8,128)} %map_hbm.1, bf16[2,1,8,1,512,128]{5,4,3,2,1,0:T(8,128)(2,1)} %lesser.1, bf16[2,16,512,128]{3,2,1,0:T(8,128)(2,1)} %coupling.1), custom_call_target="tpu_custom_call" | custom-call | tf_op jit(solution)/shard_map/pallas_call | solution.py:319
  89.4 1.3 %copy.5 = bf16[2,4,8,1,128,128]{5,4,3,2,1,0:T(8,128)(2,1)} copy(bf16[2,4,8,1,128,128]{5,4,3,2,1,0:T(8,128)(2,1)S(1)} %shard_map.37) | data formatting | bytes 4194304

commit v2 on v1

v2 whole, which is shorter than its diff:
```python
import functools

import jax
import jax.numpy as jnp
from jax import lax
from jax.experimental import pallas as pl
from jax.experimental.pallas import tpu as pltpu
from jax.sharding import PartitionSpec as P

MESH = pl.DeviceIdType.MESH
LEAD, RELAY, EARLY, DIAG, LATE = 3, 2, 3, 4, 5
SLOTS = 8
GROUPS = 2
PACE = 5


def complex_terms(green, selected):
    real_out = jnp.einsum(
        "prm,tpmj->trj", green[0], selected[0], preferred_element_type=jnp.float32
    ) - jnp.einsum("prm,tpmj->trj", green[1], selected[1], preferred_element_type=jnp.float32)
    imag_out = jnp.einsum(
        "prm,tpmj->trj", green[0], selected[1], preferred_element_type=jnp.float32
    ) + jnp.einsum("prm,tpmj->trj", green[1], selected[0], preferred_element_type=jnp.float32)
    return (real_out, imag_out)


def per_device_general(lesser, coupling, transfer_map):
    regrouped = lax.all_to_all(lesser, "energy", split_axis=4, concat_axis=1, tiled=True)
    gathered = lax.all_gather(regrouped, "orb", axis=5, tiled=True)
    energies = gathered.shape[1]
    local_points = gathered.shape[2]
    layers = gathered.shape[3]
    tile = gathered.shape[4]
    width = gathered.shape[5]
    out_cols = coupling.shape[3]
    row_count = energies * layers * tile
    first_point = lax.axis_index("kpt") * local_points
    reordered = jnp.moveaxis(gathered, 2, 1).reshape(2, local_points, row_count, width)
    my_columns = lax.dynamic_slice_in_dim(transfer_map, first_point, local_points, 1)
    selected = jnp.take(coupling, my_columns, axis=1)
    real_out, imag_out = complex_terms(reordered, selected)
    mine = lax.psum_scatter(
        jnp.stack([real_out, imag_out], axis=1), "kpt", scatter_dimension=0, tiled=True
    )
    summed = jnp.moveaxis(mine, 1, 0)
    result = summed.astype(jnp.bfloat16).reshape(2, local_points, energies, layers, tile, out_cols)
    return jnp.moveaxis(result, 1, 2)


def kernel(nz, map_hbm, lesser, coupling, out, g, u, acc, map_ref, sems, zsend, zrecv, far, local_sem, u_sem, map_sem):
    osend, orecv, fsend, frecv, psend, precv, qrecv = (sems.at[n] for n in range(7))
    points = lesser.shape[2]
    width = lesser.shape[5]
    tile = g.shape[5]
    ticks = nz * points
    bunch = points // GROUPS
    e = lax.axis_index("energy")
    o = lax.axis_index("orb")
    c = lax.axis_index("kpt")
    ox = o + 1 - 2 * lax.rem(o, 2)
    oy = lax.rem(o + 2, 4)
    od = 3 - o
    cp = 1 - c
    to_x, to_y, to_peer = {"orb": ox}, {"orb": oy}, {"kpt": cp}

    def phase(i):
        return lax.div(i, points)

    def point(i):
        return lax.rem(i, points)

    def slot(i):
        return lax.rem(i, SLOTS)

    def offset(p):
        near = lax.div(p + 1, 2)
        return lax.select(lax.rem(p, 2) == 1, near, lax.rem(nz - lax.div(p, 2), nz))

    def owner(i):
        return lax.rem(e + nz - offset(phase(i)), nz)

    def rows(z):
        return pl.ds(pl.multiple_of(z * tile, tile), tile)

    def block(k, q, i):
        return g.at[k, q, :, point(i), owner(i)]

    def remote(src, dst, send_sem, recv_sem, target):
        return pltpu.make_async_remote_copy(
            src_ref=src,
            dst_ref=dst,
            send_sem=send_sem,
            recv_sem=recv_sem,
            device_id=target,
            device_id_type=MESH,
        )

    def z_copy(n):
        p = lax.div(n, GROUPS) + 1
        some = pl.ds(lax.rem(n, GROUPS) * bunch, bunch)
        target = lax.rem(e + offset(p), nz)
        return remote(
            lesser.at[:, 0, some, 0, rows(target), :],
            g.at[c, o, :, some, e],
            zsend.at[n],
            zrecv.at[n],
            {"energy": target},
        )

    def z_arrival(n):
        p = lax.div(n, GROUPS) + 1
        some = pl.ds(lax.rem(n, GROUPS) * bunch, bunch)
        source = lax.rem(e + nz - offset(p), nz)
        ref = g.at[c, o, :, some, source]
        return remote(ref, ref, zsend.at[n], zrecv.at[n], {"energy": source})

    local_copy = pltpu.make_async_copy(
        lesser.at[:, 0, :, 0, rows(e), :], g.at[c, o, :, :, e], local_sem
    )

    def own_start(i, src):
        for target in (to_x, to_y):
            remote(src, block(c, o, i), osend.at[slot(i)], orecv.at[slot(i)], target).start()

    def own_both(i):
        ref = g.at[c, pl.ds(0, 2), :, point(i), owner(i)]
        return remote(ref, ref, osend.at[slot(i)], orecv.at[slot(i)], to_x)

    def relay_start(i):
        for part, q, target in ((0, ox, to_y), (1, oy, to_x)):
            ref = g.at[c, q, part, point(i), owner(i)]
            remote(ref, ref, fsend.at[slot(i)], frecv.at[slot(i)], target).start()

    def relay_both(i):
        ref = block(c, od, i)
        return remote(ref, ref, fsend.at[slot(i)], frecv.at[slot(i)], to_x)

    def peer_start(i, q, recv):
        ref = block(c, q, i)
        remote(ref, ref, psend.at[slot(i)], recv.at[slot(i)], to_peer).start()

    def peer_some(i, count, recv):
        ref = g.at[cp, pl.ds(0, count), :, point(i), owner(i)]
        return remote(ref, ref, psend.at[slot(i)], recv.at[slot(i)], to_peer)

    barrier = pltpu.get_barrier_semaphore()
    has_low, has_high = e > 0, e < nz - 1
    for target in (to_x, to_y, to_peer):
        pl.semaphore_signal(barrier, inc=1, device_id=target, device_id_type=MESH)

    def signal(sem, target, wanted):
        @pl.when(wanted)
        def _():
            pl.semaphore_signal(sem, inc=1, device_id={"energy": target}, device_id_type=MESH)

    signal(barrier, e - 1, has_low)
    signal(barrier, e + 1, has_high)
    local_copy.start()
    map_copy = pltpu.make_async_copy(map_hbm, map_ref, map_sem)
    map_copy.start()
    u_copy = pltpu.make_async_copy(coupling, u, u_sem)
    u_copy.start()
    pl.semaphore_wait(barrier, 3 + has_low.astype(jnp.int32) + has_high.astype(jnp.int32))

    for i in range(LEAD):
        own_start(i, lesser.at[:, 0, i, 0, rows(e), :])

    for h in range(nz - 2):
        signal(far.at[0, h], e - 1, has_low & (e + h + 1 < nz))
        signal(far.at[1, h], e + 1, has_high & (e - h - 1 >= 0))

        @pl.when(e + h + 2 < nz)
        def _(h=h):
            pl.semaphore_wait(far.at[0, h], 1)

        @pl.when(e - h - 2 >= 0)
        def _(h=h):
            pl.semaphore_wait(far.at[1, h], 1)

    def z_start(n, _):
        z_copy(n).start()
        return 0

    z_groups = (nz - 1) * GROUPS
    lax.fori_loop(0, GROUPS, z_start, 0)
    acc[...] = jnp.zeros(acc.shape, acc.dtype)
    local_copy.wait()
    map_copy.wait()
    u_copy.wait()

    def multiply(chunks, i, store):
        s = point(i)
        z = owner(i)
        half = lax.rem(phase(i), 2)

        def one(t, _):
            lhs, rhs = [], []
            for k, q in chunks:
                lhs.append(g[k, q, 0, s, z])
                lhs.append(g[k, q, 1, s, z])
                index = map_ref[c * points + t, k * points + s]
                at = pl.ds(pl.multiple_of(q * width, width), width)
                ur = u[0, index, at, :]
                ui = u[1, index, at, :]
                rhs.append(jnp.concatenate([ur, ui], axis=1))
                rhs.append(jnp.concatenate([-ui, ur], axis=1))
            product = jnp.dot(
                jnp.concatenate(lhs, axis=1),
                jnp.concatenate(rhs, axis=0),
                preferred_element_type=jnp.float32,
            )
            store(half, z, t, acc[half, t] + product)
            return 0

        lax.fori_loop(0, points, one, 0, unroll=True)

    def add(half, z, t, values):
        acc[half, t] = values

    def write(half, z, t, values):
        for part in range(2):
            out[part, z, t, 0] = values[:, part * width : (part + 1) * width].astype(out.dtype)

    early = ((c, o), (cp, o), (c, ox), (cp, ox), (c, oy), (cp, oy))
    late = ((c, od), (cp, od))

    def lagged(i, lag):
        return pl.when((i >= lag) & (i < ticks + lag))

    def drain(r):
        own_both(r).wait_send()
        relay_both(r).wait_send()
        peer_some(r, 4, precv).wait_send()

    def tick(i, _):
        @pl.when((i > 0) & (i <= (nz - 2) * PACE) & (lax.rem(i, PACE) == 0))
        def _():
            n = lax.div(i, PACE) * GROUPS
            lax.fori_loop(n, n + GROUPS, z_start, 0)

        @pl.when((i >= points) & (i < ticks) & (lax.rem(i, bunch) == 0))
        def _():
            z_arrival(lax.div(i - points, bunch)).wait_recv()

        @pl.when((i >= LEAD) & (i < ticks))
        def _():
            own_start(i, block(c, o, i))

        @lagged(i, 0)
        def _():
            peer_start(i, o, precv)

        @lagged(i, RELAY)
        def _():
            r = i - RELAY
            own_both(r).wait_recv()
            relay_start(r)
            peer_start(r, ox, precv)
            peer_start(r, oy, precv)

        @lagged(i, DIAG)
        def _():
            r = i - DIAG
            relay_both(r).wait_recv()
            peer_start(r, od, qrecv)

        @lagged(i, EARLY)
        def _():
            r = i - EARLY
            peer_some(r, 3, precv).wait_recv()
            multiply(early, r, add)

        @pl.when(i >= LATE)
        def _():
            r = i - LATE
            peer_some(r, 1, qrecv).wait_recv()
            multiply(late, r, add)
            drain(r)

            @pl.when(point(r) == points - 1)
            def _():
                half = lax.rem(phase(r), 2)

                def flush(t, _):
                    write(half, owner(r), t, acc[half, t])
                    acc[half, t] = jnp.zeros(acc.shape[2:], acc.dtype)
                    return 0

                lax.fori_loop(0, points, flush, 0, unroll=True)

        return 0

    lax.fori_loop(0, ticks + LATE - 1, tick, 0)
    last = ticks - 1
    peer_some(last, 1, qrecv).wait_recv()
    multiply(late, last, write)
    drain(last)

    def z_drain(n, _):
        z_copy(n).wait_send()
        return 0

    lax.fori_loop(0, z_groups, z_drain, 0)


def per_device_fused(nz, lesser, coupling, transfer_map):
    points = lesser.shape[2]
    tile = lesser.shape[4] // nz
    width = lesser.shape[5]
    out_cols = coupling.shape[3]
    dma = pltpu.SemaphoreType.DMA
    lesser, coupling, transfer_map = (
        pltpu.with_memory_space_constraint(x, pltpu.HBM) for x in (lesser, coupling, transfer_map)
    )
    return pl.pallas_call(
        functools.partial(kernel, nz),
        out_shape=jax.ShapeDtypeStruct((2, nz, points, 1, tile, out_cols), jnp.bfloat16),
        in_specs=[pl.BlockSpec(memory_space=pltpu.HBM)] * 3,
        out_specs=pl.BlockSpec(memory_space=pltpu.VMEM),
        scratch_shapes=[
            pltpu.VMEM((2, 4, 2, points, nz, tile, width), lesser.dtype),
            pltpu.VMEM(coupling.shape, coupling.dtype),
            pltpu.VMEM((2, points, tile, 2 * out_cols), jnp.float32),
            pltpu.SMEM(transfer_map.shape, transfer_map.dtype),
            dma((7, SLOTS)),
            dma(((nz - 1) * GROUPS,)),
            dma(((nz - 1) * GROUPS,)),
            pltpu.SemaphoreType.REGULAR((2, max(nz - 2, 1))),
            dma(()),
            dma(()),
            dma(()),
        ],
        compiler_params=pltpu.CompilerParams(
            collective_id=0, has_side_effects=True, vmem_limit_bytes=40 * 1024 * 1024
        ),
    )(transfer_map, lesser, coupling)


def solution(mesh):
    in_specs = (P(None, "energy", "kpt", None, None, "orb"), P(None, None, None, "orb"), P())
    out_specs = P(None, None, "kpt", None, "energy", "orb")
    nz = mesh.shape["energy"]

    def per_device(lesser, coupling, transfer_map):
        shape = lesser.shape
        fused = (
            mesh.shape["orb"] == 4
            and mesh.shape["kpt"] == 2
            and nz > 1
            and shape[1] == 1
            and shape[3] == 1
            and shape[5] == coupling.shape[3] == 128
            and shape[4] == nz * 128
            and shape[2] % GROUPS == 0
            and nz * shape[2] > LEAD
            and PACE <= shape[2]
        )
        if fused:
            return per_device_fused(nz, lesser, coupling, transfer_map)
        return per_device_general(lesser, coupling, transfer_map)

    return jax.shard_map(
        per_device, mesh=mesh, in_specs=in_specs, out_specs=out_specs, check_vma=False
    )
```

time: 90.9 us -> 78.4 us (0.86)
  Pallas kernels: 89.4 us -> 76.7 us
    pallas_call x1, Pallas kernels: 89.4 us -> 76.7 us  [per_device_fused(): pl.pallas_call(functools.partial(kernel, nz), out_shape=jax.ShapeDtypeStr...]
where the time goes in v2:
time: 78.4 us; the launch traced here: 78 us
  Pallas kernels  76.7 us (98%)
  local copies, waits for them, and re-layouts  1.32 us (2%)
    pallas_call x1, Pallas kernels, per_device_fused(): pl.pallas_call(functools.partial(kernel, nz), out_shape=jax.ShapeDtypeStr...  76.7 us

profile of v2, /device:TPU:0, one launch (start us, length us, event | category | flops | bytes accessed | tf_op | source)
XLA Modules:
  0.0 78.0 jit_solution(2977965635002568942)
XLA Ops:
  0.0 76.7 %shard_map.37 = bf16[2,4,8,1,128,128]{5,4,3,2,1,0:T(8,128)(2,1)S(1)} custom-call(s32[16,16]{1,0:T(8,128)} %map_hbm.1, bf16[2,1,8,1,512,128]{5,4,3,2,1,0:T(8,128)(2,1)} %lesser.1, bf16[2,16,512,128]{3,2,1,0:T(8,128)(2,1)} %coupling.1), custom_call_target="tpu_custom_call" | custom-call | tf_op jit(solution)/shard_map/pallas_call | solution.py:315
  76.7 1.3 %copy.5 = bf16[2,4,8,1,128,128]{5,4,3,2,1,0:T(8,128)(2,1)} copy(bf16[2,4,8,1,128,128]{5,4,3,2,1,0:T(8,128)(2,1)S(1)} %shard_map.37) | data formatting | bytes 4194304

commit v3 on v2

--- a/solution.py
+++ b/solution.py
@@ -8,7 +8,9 @@
 from jax.sharding import PartitionSpec as P
 
 MESH = pl.DeviceIdType.MESH
-LEAD, RELAY, EARLY, DIAG, LATE = 3, 2, 3, 4, 5
+LEAD, RELAY, EARLY, DIAG, LATE = 4, 2, 3, 5, 6
+ADVANCE = 26
+CATCH_UP = 12
 SLOTS = 8
 GROUPS = 2
 PACE = 5
@@ -48,10 +50,11 @@
 
 
 def kernel(nz, map_hbm, lesser, coupling, out, g, u, acc, map_ref, sems, zsend, zrecv, far, local_sem, u_sem, map_sem):
-    osend, orecv, fsend, frecv, psend, precv, qrecv = (sems.at[n] for n in range(7))
+    sent, orecv, frecv, precv, qrecv = (sems.at[n] for n in range(5))
     points = lesser.shape[2]
     width = lesser.shape[5]
     tile = g.shape[5]
+    copies = 7
     ticks = nz * points
     bunch = points // GROUPS
     e = lax.axis_index("energy")
@@ -83,7 +86,7 @@
         return pl.ds(pl.multiple_of(z * tile, tile), tile)
 
     def block(k, q, i):
-        return g.at[k, q, :, point(i), owner(i)]
+        return g.at[k, q, point(i), owner(i)]
 
     def remote(src, dst, send_sem, recv_sem, target):
         return pltpu.make_async_remote_copy(
@@ -95,53 +98,62 @@
             device_id_type=MESH,
         )
 
-    def z_copy(n):
+    def z_start(n, _):
         p = lax.div(n, GROUPS) + 1
         some = pl.ds(lax.rem(n, GROUPS) * bunch, bunch)
         target = lax.rem(e + offset(p), nz)
-        return remote(
-            lesser.at[:, 0, some, 0, rows(target), :],
-            g.at[c, o, :, some, e],
-            zsend.at[n],
-            zrecv.at[n],
-            {"energy": target},
+        for part in range(2):
+            remote(
+                lesser.at[part, 0, some, 0, rows(target), :],
+                g.at[c, o, some, e, part],
+                zsend,
+                zrecv.at[n],
+                {"energy": target},
+            ).start()
+        return 0
+
+    def z_arrival(n):
+        ref = g.at[c, o, pl.ds(0, bunch), 0]
+        return remote(ref, ref, zsend, zrecv.at[n], to_x)
+
+    def z_sent():
+        ref = g.at[c, pl.ds(0, nz - 1), :, 0]
+        return remote(ref, ref, zsend, zrecv.at[0], to_x)
+
+    def local_copy(part):
+        return pltpu.make_async_copy(
+            lesser.at[part, 0, :, 0, rows(e), :], g.at[c, o, :, e, part], local_sem.at[part]
         )
 
-    def z_arrival(n):
-        p = lax.div(n, GROUPS) + 1
-        some = pl.ds(lax.rem(n, GROUPS) * bunch, bunch)
-        source = lax.rem(e + nz - offset(p), nz)
-        ref = g.at[c, o, :, some, source]
-        return remote(ref, ref, zsend.at[n], zrecv.at[n], {"energy": source})
-
-    local_copy = pltpu.make_async_copy(
-        lesser.at[:, 0, :, 0, rows(e), :], g.at[c, o, :, :, e], local_sem
-    )
-
-    def own_start(i, src):
+    def own_start(i):
+        ref = block(c, o, i)
         for target in (to_x, to_y):
-            remote(src, block(c, o, i), osend.at[slot(i)], orecv.at[slot(i)], target).start()
+            remote(ref, ref, sent.at[slot(i)], orecv.at[slot(i)], target).start()
 
     def own_both(i):
-        ref = g.at[c, pl.ds(0, 2), :, point(i), owner(i)]
-        return remote(ref, ref, osend.at[slot(i)], orecv.at[slot(i)], to_x)
+        ref = g.at[c, pl.ds(0, 2), point(i), owner(i)]
+        return remote(ref, ref, sent.at[slot(i)], orecv.at[slot(i)], to_x)
 
     def relay_start(i):
         for part, q, target in ((0, ox, to_y), (1, oy, to_x)):
-            ref = g.at[c, q, part, point(i), owner(i)]
-            remote(ref, ref, fsend.at[slot(i)], frecv.at[slot(i)], target).start()
+            ref = g.at[c, q, point(i), owner(i), part]
+            remote(ref, ref, sent.at[slot(i)], frecv.at[slot(i)], target).start()
 
     def relay_both(i):
         ref = block(c, od, i)
-        return remote(ref, ref, fsend.at[slot(i)], frecv.at[slot(i)], to_x)
+        return remote(ref, ref, sent.at[slot(i)], frecv.at[slot(i)], to_x)
+
+    def all_sent(i):
+        ref = g.at[c, o, pl.ds(0, copies), 0]
+        return remote(ref, ref, sent.at[slot(i)], orecv.at[slot(i)], to_x)
 
     def peer_start(i, q, recv):
         ref = block(c, q, i)
-        remote(ref, ref, psend.at[slot(i)], recv.at[slot(i)], to_peer).start()
+        remote(ref, ref, sent.at[slot(i)], recv.at[slot(i)], to_peer).start()
 
     def peer_some(i, count, recv):
-        ref = g.at[cp, pl.ds(0, count), :, point(i), owner(i)]
-        return remote(ref, ref, psend.at[slot(i)], recv.at[slot(i)], to_peer)
+        ref = g.at[cp, pl.ds(0, count), point(i), owner(i)]
+        return remote(ref, ref, sent.at[slot(i)], recv.at[slot(i)], to_peer)
 
     barrier = pltpu.get_barrier_semaphore()
     has_low, has_high = e > 0, e < nz - 1
@@ -155,15 +167,19 @@
 
     signal(barrier, e - 1, has_low)
     signal(barrier, e + 1, has_high)
-    local_copy.start()
+    for part in range(2):
+        local_copy(part).start()
     map_copy = pltpu.make_async_copy(map_hbm, map_ref, map_sem)
     map_copy.start()
     u_copy = pltpu.make_async_copy(coupling, u, u_sem)
     u_copy.start()
     pl.semaphore_wait(barrier, 3 + has_low.astype(jnp.int32) + has_high.astype(jnp.int32))
 
+    for part in range(2):
+        local_copy(part).wait()
     for i in range(LEAD):
-        own_start(i, lesser.at[:, 0, i, 0, rows(e), :])
+        own_start(i)
+        peer_start(i, o, precv)
 
     for h in range(nz - 2):
         signal(far.at[0, h], e - 1, has_low & (e + h + 1 < nz))
@@ -177,14 +193,8 @@
         def _(h=h):
             pl.semaphore_wait(far.at[1, h], 1)
 
-    def z_start(n, _):
-        z_copy(n).start()
-        return 0
-
-    z_groups = (nz - 1) * GROUPS
     lax.fori_loop(0, GROUPS, z_start, 0)
     acc[...] = jnp.zeros(acc.shape, acc.dtype)
-    local_copy.wait()
     map_copy.wait()
     u_copy.wait()
 
@@ -196,8 +206,8 @@
         def one(t, _):
             lhs, rhs = [], []
             for k, q in chunks:
-                lhs.append(g[k, q, 0, s, z])
-                lhs.append(g[k, q, 1, s, z])
+                lhs.append(g[k, q, s, z, 0])
+                lhs.append(g[k, q, s, z, 1])
                 index = map_ref[c * points + t, k * points + s]
                 at = pl.ds(pl.multiple_of(q * width, width), width)
                 ur = u[0, index, at, :]
@@ -221,16 +231,38 @@
         for part in range(2):
             out[part, z, t, 0] = values[:, part * width : (part + 1) * width].astype(out.dtype)
 
-    early = ((c, o), (cp, o), (c, ox), (cp, ox), (c, oy), (cp, oy))
-    late = ((c, od), (cp, od))
-
-    def lagged(i, lag):
-        return pl.when((i >= lag) & (i < ticks + lag))
-
-    def drain(r):
-        own_both(r).wait_send()
-        relay_both(r).wait_send()
-        peer_some(r, 4, precv).wait_send()
+    near_chunks = ((c, o), (cp, o), (c, ox), (cp, ox), (c, oy), (cp, oy))
+    far_chunks = ((c, od), (cp, od))
+
+    def relay(r):
+        own_both(r).wait_recv()
+        relay_start(r)
+        peer_start(r, ox, precv)
+        peer_start(r, oy, precv)
+
+    def diagonal(r):
+        relay_both(r).wait_recv()
+        peer_start(r, od, qrecv)
+
+    def early(r):
+        peer_some(r, 3, precv).wait_recv()
+        multiply(near_chunks, r, add)
+
+    def late(r):
+        peer_some(r, 1, qrecv).wait_recv()
+        multiply(far_chunks, r, add)
+        all_sent(r).wait_send()
+
+        @pl.when(point(r) == points - 1)
+        def _():
+            half = lax.rem(phase(r), 2)
+
+            def flush(t, _):
+                write(half, owner(r), t, acc[half, t])
+                acc[half, t] = jnp.zeros(acc.shape[2:], acc.dtype)
+                return 0
+
+            lax.fori_loop(0, points, flush, 0, unroll=True)
 
     def tick(i, _):
         @pl.when((i > 0) & (i <= (nz - 2) * PACE) & (lax.rem(i, PACE) == 0))
@@ -238,69 +270,58 @@
             n = lax.div(i, PACE) * GROUPS
             lax.fori_loop(n, n + GROUPS, z_start, 0)
 
-        @pl.when((i >= points) & (i < ticks) & (lax.rem(i, bunch) == 0))
-        def _():
-            z_arrival(lax.div(i - points, bunch)).wait_recv()
-
-        @pl.when((i >= LEAD) & (i < ticks))
-        def _():
-            own_start(i, block(c, o, i))
-
-        @lagged(i, 0)
-        def _():
-            peer_start(i, o, precv)
-
-        @lagged(i, RELAY)
-        def _():
-            r = i - RELAY
-            own_both(r).wait_recv()
-            relay_start(r)
-            peer_start(r, ox, precv)
-            peer_start(r, oy, precv)
-
-        @lagged(i, DIAG)
-        def _():
-            r = i - DIAG
-            relay_both(r).wait_recv()
-            peer_start(r, od, qrecv)
-
-        @lagged(i, EARLY)
-        def _():
-            r = i - EARLY
-            peer_some(r, 3, precv).wait_recv()
-            multiply(early, r, add)
+        def own(j, _):
+            @pl.when((j >= points) & (lax.rem(j, bunch) == 0))
+            def _():
+                z_arrival(lax.div(j - points, bunch)).wait_recv()
+
+            own_start(j)
+            peer_start(j, o, precv)
+            return 0
+
+        def lead(j):
+            return lax.max(lax.min(j + (j >= ADVANCE).astype(jnp.int32), ticks), LEAD)
+
+        lax.fori_loop(lead(i), lead(i + 1), own, 0)
+
+        @pl.when(i >= RELAY)
+        def _():
+            relay(i - RELAY)
+
+        @pl.when(i >= DIAG)
+        def _():
+            diagonal(i - DIAG)
+
+        def one(r, _):
+            early(r)
+            return 0
+
+        slow, slow_next = ((j < CATCH_UP).astype(jnp.int32) for j in (i, i + 1))
+        lax.fori_loop(lax.max(i - EARLY - slow, 0), lax.max(i + 1 - EARLY - slow_next, 0), one, 0)
 
         @pl.when(i >= LATE)
         def _():
-            r = i - LATE
-            peer_some(r, 1, qrecv).wait_recv()
-            multiply(late, r, add)
-            drain(r)
-
-            @pl.when(point(r) == points - 1)
-            def _():
-                half = lax.rem(phase(r), 2)
-
-                def flush(t, _):
-                    write(half, owner(r), t, acc[half, t])
-                    acc[half, t] = jnp.zeros(acc.shape[2:], acc.dtype)
-                    return 0
-
-                lax.fori_loop(0, points, flush, 0, unroll=True)
+            late(i - LATE)
 
         return 0
 
-    lax.fori_loop(0, ticks + LATE - 1, tick, 0)
+    lax.fori_loop(0, ticks + 1, tick, 0)
     last = ticks - 1
+    relay(last)
+    early(last - 1)
+    diagonal(last - 3)
+    late(last - 4)
+    diagonal(last - 2)
+    late(last - 3)
+    diagonal(last - 1)
+    early(last)
+    diagonal(last)
+    late(last - 2)
+    late(last - 1)
     peer_some(last, 1, qrecv).wait_recv()
-    multiply(late, last, write)
-    drain(last)
-
-    def z_drain(n, _):
-        z_copy(n).wait_send()
-        return 0
-
-    lax.fori_loop(0, z_groups, z_drain, 0)
+    multiply(far_chunks, last, write)
+    all_sent(last).wait_send()
+    z_sent().wait_send()
 
 
 def per_device_fused(nz, lesser, coupling, transfer_map):
@@ -318,15 +339,15 @@
         in_specs=[pl.BlockSpec(memory_space=pltpu.HBM)] * 3,
         out_specs=pl.BlockSpec(memory_space=pltpu.VMEM),
         scratch_shapes=[
-            pltpu.VMEM((2, 4, 2, points, nz, tile, width), lesser.dtype),
+            pltpu.VMEM((2, 4, points, nz, 2, tile, width), lesser.dtype),
             pltpu.VMEM(coupling.shape, coupling.dtype),
             pltpu.VMEM((2, points, tile, 2 * out_cols), jnp.float32),
             pltpu.SMEM(transfer_map.shape, transfer_map.dtype),
-            dma((7, SLOTS)),
-            dma(((nz - 1) * GROUPS,)),
+            dma((5, SLOTS)),
+            dma(()),
             dma(((nz - 1) * GROUPS,)),
             pltpu.SemaphoreType.REGULAR((2, max(nz - 2, 1))),
-            dma(()),
+            dma((2,)),
             dma(()),
             dma(()),
         ],
@@ -352,8 +373,10 @@
             and shape[5] == coupling.shape[3] == 128
             and shape[4] == nz * 128
             and shape[2] % GROUPS == 0
-            and nz * shape[2] > LEAD
-            and PACE <= shape[2]
+            and shape[2] % 2 == 0
+            and shape[2] >= 8
+            and nz <= 5
+            and nz * shape[2] > max(CATCH_UP, ADVANCE)
         )
         if fused:
             return per_device_fused(nz, lesser, coupling, transfer_map)

time: 78.4 us -> 77.3 us (0.986)
  Pallas kernels: 76.7 us -> 75.8 us
    pallas_call x1, Pallas kernels: 76.7 us -> 75.8 us  [per_device_fused(): pl.pallas_call(functools.partial(kernel, nz), out_shape=jax.ShapeDtypeStr...]
where the time goes in v3:
time: 77.3 us; the launch traced here: 77.1 us
  Pallas kernels  75.8 us (98%)
  local copies, waits for them, and re-layouts  1.32 us (2%)
    pallas_call x1, Pallas kernels, per_device_fused(): pl.pallas_call(functools.partial(kernel, nz), out_shape=jax.ShapeDtypeStr...  75.8 us

profile of v3, /device:TPU:0, one launch (start us, length us, event | category | flops | bytes accessed | tf_op | source)
XLA Modules:
  0.0 77.1 jit_solution(2300999244352840112)
XLA Ops:
  0.0 75.8 %shard_map.37 = bf16[2,4,8,1,128,128]{5,4,3,2,1,0:T(8,128)(2,1)S(1)} custom-call(s32[16,16]{1,0:T(8,128)} %map_hbm.1, bf16[2,1,8,1,512,128]{5,4,3,2,1,0:T(8,128)(2,1)} %lesser.1, bf16[2,16,512,128]{3,2,1,0:T(8,128)(2,1)} %coupling.1), custom_call_target="tpu_custom_call" | custom-call | tf_op jit(solution)/shard_map/pallas_call | solution.py:336
  75.8 1.3 %copy.5 = bf16[2,4,8,1,128,128]{5,4,3,2,1,0:T(8,128)(2,1)} copy(bf16[2,4,8,1,128,128]{5,4,3,2,1,0:T(8,128)(2,1)S(1)} %shard_map.37) | data formatting | bytes 4194304

commit v4 on v3

--- a/solution.py
+++ b/solution.py
@@ -9,9 +9,11 @@
 
 MESH = pl.DeviceIdType.MESH
 LEAD, RELAY, EARLY, DIAG, LATE = 4, 2, 3, 5, 6
-ADVANCE = 26
+ADVANCE = (24,27)
+DEEPER = 25
 CATCH_UP = 12
-SLOTS = 8
+SLOTS = 10
+FIRST = 2
 GROUPS = 2
 PACE = 5
 
@@ -49,8 +51,8 @@
     return jnp.moveaxis(result, 1, 2)
 
 
-def kernel(nz, map_hbm, lesser, coupling, out, g, u, acc, map_ref, sems, zsend, zrecv, far, local_sem, u_sem, map_sem):
-    sent, orecv, frecv, precv, qrecv = (sems.at[n] for n in range(5))
+def kernel(nz, map_hbm, lesser, coupling, out, g, u, acc, map_ref, sems, sent, zsend, zrecv, far, local_sem, u_sem, map_sem):
+    orecv, frecv, precv, qrecv = (sems.at[n] for n in range(4))
     points = lesser.shape[2]
     width = lesser.shape[5]
     tile = g.shape[5]
@@ -120,40 +122,49 @@
         ref = g.at[c, pl.ds(0, nz - 1), :, 0]
         return remote(ref, ref, zsend, zrecv.at[0], to_x)
 
-    def local_copy(part):
-        return pltpu.make_async_copy(
-            lesser.at[part, 0, :, 0, rows(e), :], g.at[c, o, :, e, part], local_sem.at[part]
-        )
+    pieces = (pl.ds(0, FIRST), pl.ds(FIRST, points - FIRST))
+
+    def local_start(n):
+        for part in range(2):
+            pltpu.make_async_copy(
+                lesser.at[part, 0, pieces[n], 0, rows(e), :],
+                g.at[c, o, pieces[n], e, part],
+                local_sem.at[n],
+            ).start()
+
+    def local_wait(n):
+        ref = g.at[c, o, pieces[n], e]
+        pltpu.make_async_copy(ref, ref, local_sem.at[n]).wait()
 
     def own_start(i):
         ref = block(c, o, i)
         for target in (to_x, to_y):
-            remote(ref, ref, sent.at[slot(i)], orecv.at[slot(i)], target).start()
+            remote(ref, ref, sent, orecv.at[slot(i)], target).start()
 
     def own_both(i):
         ref = g.at[c, pl.ds(0, 2), point(i), owner(i)]
-        return remote(ref, ref, sent.at[slot(i)], orecv.at[slot(i)], to_x)
+        return remote(ref, ref, sent, orecv.at[slot(i)], to_x)
 
     def relay_start(i):
         for part, q, target in ((0, ox, to_y), (1, oy, to_x)):
             ref = g.at[c, q, point(i), owner(i), part]
-            remote(ref, ref, sent.at[slot(i)], frecv.at[slot(i)], target).start()
+            remote(ref, ref, sent, frecv.at[slot(i)], target).start()
 
     def relay_both(i):
         ref = block(c, od, i)
-        return remote(ref, ref, sent.at[slot(i)], frecv.at[slot(i)], to_x)
-
-    def all_sent(i):
-        ref = g.at[c, o, pl.ds(0, copies), 0]
-        return remote(ref, ref, sent.at[slot(i)], orecv.at[slot(i)], to_x)
+        return remote(ref, ref, sent, frecv.at[slot(i)], to_x)
+
+    def all_sent():
+        ref = g.at[:, :, :, :, :, pl.ds(0, tile * copies // 8), :]
+        return remote(ref, ref, sent, orecv.at[0], to_x)
 
     def peer_start(i, q, recv):
         ref = block(c, q, i)
-        remote(ref, ref, sent.at[slot(i)], recv.at[slot(i)], to_peer).start()
+        remote(ref, ref, sent, recv.at[slot(i)], to_peer).start()
 
     def peer_some(i, count, recv):
         ref = g.at[cp, pl.ds(0, count), point(i), owner(i)]
-        return remote(ref, ref, sent.at[slot(i)], recv.at[slot(i)], to_peer)
+        return remote(ref, ref, sent, recv.at[slot(i)], to_peer)
 
     barrier = pltpu.get_barrier_semaphore()
     has_low, has_high = e > 0, e < nz - 1
@@ -167,17 +178,18 @@
 
     signal(barrier, e - 1, has_low)
     signal(barrier, e + 1, has_high)
-    for part in range(2):
-        local_copy(part).start()
+    for n in range(2):
+        local_start(n)
     map_copy = pltpu.make_async_copy(map_hbm, map_ref, map_sem)
     map_copy.start()
     u_copy = pltpu.make_async_copy(coupling, u, u_sem)
     u_copy.start()
     pl.semaphore_wait(barrier, 3 + has_low.astype(jnp.int32) + has_high.astype(jnp.int32))
 
-    for part in range(2):
-        local_copy(part).wait()
+    local_wait(0)
     for i in range(LEAD):
+        if i == FIRST:
+            local_wait(1)
         own_start(i)
         peer_start(i, o, precv)
 
@@ -251,7 +263,6 @@
     def late(r):
         peer_some(r, 1, qrecv).wait_recv()
         multiply(far_chunks, r, add)
-        all_sent(r).wait_send()
 
         @pl.when(point(r) == points - 1)
         def _():
@@ -264,63 +275,70 @@
 
             lax.fori_loop(0, points, flush, 0, unroll=True)
 
+    def after(i, bound):
+        return (i >= bound).astype(jnp.int32)
+
     def tick(i, _):
+        def stage(done, work):
+            def one(r, _):
+                work(r)
+                return 0
+
+            lax.fori_loop(done(i), done(i + 1), one, 0)
+
         @pl.when((i > 0) & (i <= (nz - 2) * PACE) & (lax.rem(i, PACE) == 0))
         def _():
             n = lax.div(i, PACE) * GROUPS
             lax.fori_loop(n, n + GROUPS, z_start, 0)
 
-        def own(j, _):
+        def own(j):
             @pl.when((j >= points) & (lax.rem(j, bunch) == 0))
             def _():
                 z_arrival(lax.div(j - points, bunch)).wait_recv()
 
             own_start(j)
             peer_start(j, o, precv)
-            return 0
-
-        def lead(j):
-            return lax.max(lax.min(j + (j >= ADVANCE).astype(jnp.int32), ticks), LEAD)
-
-        lax.fori_loop(lead(i), lead(i + 1), own, 0)
-
-        @pl.when(i >= RELAY)
-        def _():
-            relay(i - RELAY)
-
-        @pl.when(i >= DIAG)
-        def _():
-            diagonal(i - DIAG)
-
-        def one(r, _):
-            early(r)
-            return 0
-
-        slow, slow_next = ((j < CATCH_UP).astype(jnp.int32) for j in (i, i + 1))
-        lax.fori_loop(lax.max(i - EARLY - slow, 0), lax.max(i + 1 - EARLY - slow_next, 0), one, 0)
-
-        @pl.when(i >= LATE)
-        def _():
-            late(i - LATE)
-
+
+        def own_done(j):
+            return lax.max(lax.min(j + sum(after(j, a) for a in ADVANCE), ticks), LEAD)
+
+        stage(own_done, own)
+
+        def lagged(lag):
+            return lambda j: lax.max(j - lag(j), 0)
+
+        stage(lagged(lambda j: RELAY), relay)
+        stage(lagged(lambda j: DIAG + after(j, DEEPER)), diagonal)
+        stage(lagged(lambda j: EARLY + 1 - after(j, CATCH_UP)), early)
+        stage(lagged(lambda j: LATE + after(j, DEEPER)), late)
         return 0
 
-    lax.fori_loop(0, ticks + 1, tick, 0)
+    lax.fori_loop(0, ticks - 1, tick, 0)
     last = ticks - 1
+    relay(last - 2)
+    early(last - 3)
+    late(last - 7)
+    diagonal(last - 6)
+    relay(last - 1)
+    early(last - 2)
+    late(last - 6)
+    diagonal(last - 5)
     relay(last)
     early(last - 1)
+    diagonal(last - 4)
+    late(last - 5)
     diagonal(last - 3)
+    early(last)
+    diagonal(last - 2)
     late(last - 4)
-    diagonal(last - 2)
+    diagonal(last - 1)
     late(last - 3)
-    diagonal(last - 1)
-    early(last)
     diagonal(last)
     late(last - 2)
     late(last - 1)
     peer_some(last, 1, qrecv).wait_recv()
     multiply(far_chunks, last, write)
-    all_sent(last).wait_send()
+    all_sent().wait_send()
     z_sent().wait_send()
 
 
@@ -343,7 +361,8 @@
             pltpu.VMEM(coupling.shape, coupling.dtype),
             pltpu.VMEM((2, points, tile, 2 * out_cols), jnp.float32),
             pltpu.SMEM(transfer_map.shape, transfer_map.dtype),
-            dma((5, SLOTS)),
+            dma((4, SLOTS)),
+            dma(()),
             dma(()),
             dma(((nz - 1) * GROUPS,)),
             pltpu.SemaphoreType.REGULAR((2, max(nz - 2, 1))),
@@ -374,9 +393,8 @@
             and shape[4] == nz * 128
             and shape[2] % GROUPS == 0
             and shape[2] % 2 == 0
-            and shape[2] >= 8
-            and nz <= 5
-            and nz * shape[2] > max(CATCH_UP, ADVANCE)
+            and shape[2] >= max(LEAD, PACE)
+            and nz * shape[2] > max(CATCH_UP, DEEPER, LATE, *ADVANCE)
         )
         if fused:
             return per_device_fused(nz, lesser, coupling, transfer_map)

time: 77.3 us -> 76.5 us (0.990)
  Pallas kernels: 75.8 us -> 75 us
    pallas_call x1, Pallas kernels: 75.8 us -> 75 us  [per_device_fused(): pl.pallas_call(functools.partial(kernel, nz), out_shape=jax.ShapeDtypeStr...]
where the time goes in v4:
time: 76.5 us; the launch traced here: 76.3 us
  Pallas kernels  75 us (98%)
  local copies, waits for them, and re-layouts  1.32 us (2%)
    pallas_call x1, Pallas kernels, per_device_fused(): pl.pallas_call(functools.partial(kernel, nz), out_shape=jax.ShapeDtypeStr...  75 us

profile of v4, /device:TPU:0, one launch (start us, length us, event | category | flops | bytes accessed | tf_op | source)
XLA Modules:
  0.0 76.3 jit_solution(16478676503441267447)
XLA Ops:
  0.0 75.0 %shard_map.37 = bf16[2,4,8,1,128,128]{5,4,3,2,1,0:T(8,128)(2,1)S(1)} custom-call(s32[16,16]{1,0:T(8,128)} %map_hbm.1, bf16[2,1,8,1,512,128]{5,4,3,2,1,0:T(8,128)(2,1)} %lesser.1, bf16[2,16,512,128]{3,2,1,0:T(8,128)(2,1)} %coupling.1), custom_call_target="tpu_custom_call" | custom-call | tf_op jit(solution)/shard_map/pallas_call | solution.py:354
  75.0 1.3 %copy.5 = bf16[2,4,8,1,128,128]{5,4,3,2,1,0:T(8,128)(2,1)} copy(bf16[2,4,8,1,128,128]{5,4,3,2,1,0:T(8,128)(2,1)S(1)} %shard_map.37) | data formatting | bytes 4194304

commit v5 on v4

--- a/solution.py
+++ b/solution.py
@@ -8,11 +8,12 @@
 from jax.sharding import PartitionSpec as P
 
 MESH = pl.DeviceIdType.MESH
-LEAD, RELAY, EARLY, DIAG, LATE = 4, 2, 3, 5, 6
+LEAD, RELAY, EARLY, DIAG, LATE = 5, 2, 3, 5, 6
 ADVANCE = (24,27)
 DEEPER = 25
 CATCH_UP = 12
 SLOTS = 10
+DIAG_SLOTS = 6
 FIRST = 2
 GROUPS = 2
 PACE = 5
@@ -51,8 +52,8 @@
     return jnp.moveaxis(result, 1, 2)
 
 
-def kernel(nz, map_hbm, lesser, coupling, out, g, u, acc, map_ref, sems, sent, zsend, zrecv, far, local_sem, u_sem, map_sem):
-    orecv, frecv, precv, qrecv = (sems.at[n] for n in range(4))
+def kernel(nz, map_hbm, lesser, coupling, out, g, u, acc, map_ref, sems, qrecv, sent, zsend, zrecv, far, local_sem, u_sem, map_sem):
+    orecv, frecv, precv = (sems.at[n] for n in range(3))
     points = lesser.shape[2]
     width = lesser.shape[5]
     tile = g.shape[5]
@@ -158,13 +159,16 @@
         ref = g.at[:, :, :, :, :, pl.ds(0, tile * copies // 8), :]
         return remote(ref, ref, sent, orecv.at[0], to_x)
 
+    def peer_sem(i, recv):
+        return recv.at[lax.rem(i, recv.shape[0])]
+
     def peer_start(i, q, recv):
         ref = block(c, q, i)
-        remote(ref, ref, sent, recv.at[slot(i)], to_peer).start()
+        remote(ref, ref, sent, peer_sem(i, recv), to_peer).start()
 
     def peer_some(i, count, recv):
         ref = g.at[cp, pl.ds(0, count), point(i), owner(i)]
-        return remote(ref, ref, sent, recv.at[slot(i)], to_peer)
+        return remote(ref, ref, sent, peer_sem(i, recv), to_peer)
 
     barrier = pltpu.get_barrier_semaphore()
     has_low, has_high = e > 0, e < nz - 1
@@ -184,6 +188,7 @@
     map_copy.start()
     u_copy = pltpu.make_async_copy(coupling, u, u_sem)
     u_copy.start()
+    acc[...] = jnp.zeros(acc.shape, acc.dtype)
     pl.semaphore_wait(barrier, 3 + has_low.astype(jnp.int32) + has_high.astype(jnp.int32))
 
     local_wait(0)
@@ -206,7 +211,6 @@
             pl.semaphore_wait(far.at[1, h], 1)
 
     lax.fori_loop(0, GROUPS, z_start, 0)
-    acc[...] = jnp.zeros(acc.shape, acc.dtype)
     map_copy.wait()
     u_copy.wait()
 
@@ -336,8 +340,9 @@
     diagonal(last)
     late(last - 2)
     late(last - 1)
+    multiply(far_chunks[:1], last, add)
     peer_some(last, 1, qrecv).wait_recv()
-    multiply(far_chunks, last, write)
+    multiply(far_chunks[1:], last, write)
     all_sent().wait_send()
     z_sent().wait_send()
 
@@ -361,7 +366,8 @@
             pltpu.VMEM(coupling.shape, coupling.dtype),
             pltpu.VMEM((2, points, tile, 2 * out_cols), jnp.float32),
             pltpu.SMEM(transfer_map.shape, transfer_map.dtype),
-            dma((4, SLOTS)),
+            dma((3, SLOTS)),
+            dma((DIAG_SLOTS,)),
             dma(()),
             dma(()),
             dma(((nz - 1) * GROUPS,)),

time: 76.5 us -> 76.4 us (level)
  no operation moved by 1% of the time
where the time goes in v5:
time: 76.4 us; the launch traced here: 76.2 us
  Pallas kernels  74.9 us (98%)
  local copies, waits for them, and re-layouts  1.32 us (2%)
    pallas_call x1, Pallas kernels, per_device_fused(): pl.pallas_call(functools.partial(kernel, nz), out_shape=jax.ShapeDtypeStr...  74.9 us

profile of v5, /device:TPU:0, one launch (start us, length us, event | category | flops | bytes accessed | tf_op | source)
XLA Modules:
  0.0 76.2 jit_solution(15293539162898219183)
XLA Ops:
  0.0 74.9 %shard_map.37 = bf16[2,4,8,1,128,128]{5,4,3,2,1,0:T(8,128)(2,1)S(1)} custom-call(s32[16,16]{1,0:T(8,128)} %map_hbm.1, bf16[2,1,8,1,512,128]{5,4,3,2,1,0:T(8,128)(2,1)} %lesser.1, bf16[2,16,512,128]{3,2,1,0:T(8,128)(2,1)} %coupling.1), custom_call_target="tpu_custom_call" | custom-call | tf_op jit(solution)/shard_map/pallas_call | solution.py:359
  74.9 1.3 %copy.5 = bf16[2,4,8,1,128,128]{5,4,3,2,1,0:T(8,128)(2,1)} copy(bf16[2,4,8,1,128,128]{5,4,3,2,1,0:T(8,128)(2,1)S(1)} %shard_map.37) | data formatting | bytes 4194304
